TPU v7x, 32 devices: a whole 2x2x4 slice. The times are simulated.
32 devices in a mesh: groups: 1, role: 2 (over core), dev: 16 (over z, y, x).
Axes of the slice: x: 2, y: 2, z: 4, core: 2. Of those that a mesh axis runs over, the one named last changes fastest.
Arguments:
- prompt_hidden: bfloat16 [4096, 4096], P(('groups', 'dev')), may hold values from -6 to 6
- norm_gain: float32 [4096], replicated, may hold values from 0.25 to 1.75
- kv_weight: bfloat16 [4096, 4, 2, 128], P(None, 'role'), may hold values from -0.09375 to 0.09375
- prompt_excess: int32 [4], P('groups'), may hold values from 1 to 1536, 2048 in all
- prompt_owner: int32 [4], P('groups'), may hold values from 0 to 15, as said below
- response_counts: int32 [4], P('groups'), may hold values from 1 to 5, as said below
- queries: bfloat16 [256, 16, 128], P(('groups', 'dev'), 'role'), may hold values from -256 to 256
- new_kv: bfloat16 [256, 4, 2, 128], P(('groups', 'dev'), 'role'), may hold values from -6 to 6
- response_cache: bfloat16 [256, 256, 4, 2, 128], P(('groups', 'dev'), None, 'role'), may hold values from -6 to 6
- positions: int32 [256], P(('groups', 'dev')), may hold values from 0 to 256
- out_weight: bfloat16 [16, 128, 4096], P('role', None, 'dev'), may hold values from -0.125 to 0.125
Outputs:
- attended: bfloat16 [256, 16, 128], P(('groups', 'dev'), 'role')
- block_out: bfloat16 [256, 4096], P(('groups', 'role'), 'dev')
Inputs may be any that keep to these rules, and one draw needn't show every extreme that they name: `prompt_owner`: no device along dev owns more than two prompts, and some device owns exactly two. `response_counts`: some prompt has exactly 5 responses.
All inputs are finite; a program needn't handle non-finite values.
Results may differ from a plain program's by a relative error of at most 0.0065.
Values may be sent and summed in bfloat16 or wider, within the bound.
No kernel may reach another device: no remote copies, remote signals or barrier semaphores. Data moves between devices by JAX's collectives and lax.ppermute only.
A program may use at most 192 MiB of HBM per device.

v0:
```python
import jax
import jax.numpy as jnp
from jax import lax
from jax.sharding import PartitionSpec as P

RESP = 5
PROMPT_MIN = 512
rope_base = 500000.0


def merged_2(part, axis, combine):
    gathered = jax.tree.map(lambda a: lax.all_gather(a, axis), part)

    def take(source):
        return jax.tree.map(lambda a: lax.dynamic_index_in_dim(a, source, 0, False), gathered)

    return lax.fori_loop(
        1, lax.axis_size(axis), lambda source, state: combine(state, take(source)), take(0)
    )


def rotate(vectors, offsets):
    half = vectors.shape[-1] // 2
    freq = rope_base ** (-jnp.arange(half, dtype=jnp.float32) * 2.0 / vectors.shape[-1])
    angles = offsets.astype(jnp.float32)[:, None] * freq[None, :]
    cosine = jnp.cos(angles)[:, None, :]
    sine = jnp.sin(angles)[:, None, :]
    first = vectors[..., :half]
    second = vectors[..., half:]
    return jnp.concatenate(
        [first * cosine - second * sine, second * cosine + first * sine], axis=-1
    )


def prompt_layout(prompt_excess, token_index):
    lengths = PROMPT_MIN + prompt_excess
    ends = jnp.cumsum(lengths)
    starts = ends - lengths
    prompt_id = jnp.sum((token_index[:, None] >= ends[None, :]).astype(jnp.int32), axis=1)
    member = prompt_id[:, None] == jnp.arange(lengths.shape[0], dtype=jnp.int32)[None, :]
    offsets = token_index - jnp.sum(jnp.where(member, starts[None, :], 0), axis=1)
    return (member, offsets, starts, lengths)


def first_slots(owner, counts):
    order = jnp.arange(owner.shape[0], dtype=jnp.int32)
    earlier = (owner[:, None] == owner[None, :]) & (order[None, :] < order[:, None])
    return jnp.sum(jnp.where(earlier, counts[None, :], 0), axis=1)


def slot_prompts(owner, counts, slot_device, slot_index):
    order = jnp.arange(owner.shape[0], dtype=jnp.int32)
    first = first_slots(owner, counts)
    match = (
        (owner[None, :] == slot_device[:, None])
        & (first[None, :] <= slot_index[:, None])
        & (slot_index[:, None] < first[None, :] + counts[None, :])
    )
    present = jnp.any(match, axis=1)
    chosen = jnp.sum(jnp.where(match, order[None, :], 0), axis=1)
    return (chosen, present)


def softmax_state(scores, valid):
    scores = jnp.where(valid[:, None, None, :], scores, -1e30)
    peak = jnp.max(scores, axis=-1)
    weights = jnp.where(valid[:, None, None, :], jnp.exp(scores - peak[..., None]), 0.0)
    return (peak, jnp.sum(weights, axis=-1), weights.astype(jnp.bfloat16))


def state_each(query, keys, values, valid, scale):
    scores = jnp.einsum("sngd,slnd->sngl", query, keys, preferred_element_type=jnp.float32) * scale
    peak, total, rounded = softmax_state(scores, valid)
    mixed = jnp.einsum("sngl,slnd->sngd", rounded, values, preferred_element_type=jnp.float32)
    return (peak, total, mixed)


def state_shared(query, keys, values, valid, scale):
    scores = jnp.einsum("sngd,lnd->sngl", query, keys, preferred_element_type=jnp.float32) * scale
    peak, total, rounded = softmax_state(scores, valid)
    mixed = jnp.einsum("sngl,lnd->sngd", rounded, values, preferred_element_type=jnp.float32)
    return (peak, total, mixed)


def combine(first, second):
    peak = jnp.maximum(first[0], second[0])
    left_scale = jnp.exp(first[0] - peak)
    right_scale = jnp.exp(second[0] - peak)
    total = first[1] * left_scale + second[1] * right_scale
    mixed = first[2] * left_scale[..., None] + second[2] * right_scale[..., None]
    return (peak, total, mixed)


def on_device(
    prompt_hidden,
    norm_gain,
    kv_weight,
    prompt_excess,
    prompt_owner,
    response_counts,
    queries,
    new_kv,
    response_cache,
    positions,
    out_weight,
):
    device = lax.axis_index("dev")
    rows = prompt_hidden.shape[0]
    width = prompt_hidden.shape[1]
    local_heads = kv_weight.shape[1]
    head_size = kv_weight.shape[3]
    slots = queries.shape[0]
    query_heads = queries.shape[1]
    group = query_heads // local_heads
    prompt_count = prompt_excess.shape[0]
    scale = head_size ** (-0.5)
    token_index = device * rows + jnp.arange(rows, dtype=jnp.int32)
    member, offsets, starts, lengths = prompt_layout(prompt_excess, token_index)
    hidden = prompt_hidden.astype(jnp.float32)
    normed = (
        hidden * lax.rsqrt(jnp.mean(hidden * hidden, axis=-1, keepdims=True) + 1e-05) * norm_gain
    ).astype(jnp.bfloat16)
    projected = jnp.dot(
        normed,
        kv_weight.reshape(width, local_heads * 2 * head_size),
        preferred_element_type=jnp.float32,
    )
    projected = projected.reshape(rows, local_heads, 2, head_size)
    prompt_keys = rotate(projected[:, :, 0], offsets).astype(jnp.bfloat16)
    prompt_values = projected[:, :, 1].astype(jnp.bfloat16)
    grouped = queries.reshape(slots, local_heads, group, head_size)
    slot_index = jnp.arange(slots, dtype=jnp.int32)
    chosen, present = slot_prompts(
        prompt_owner, response_counts, jnp.zeros((slots,), jnp.int32) + device, slot_index
    )
    cache_valid = jnp.arange(response_cache.shape[1], dtype=jnp.int32)[None, :] < positions[:, None]
    cache_state = state_each(
        grouped, response_cache[:, :, :, 0], response_cache[:, :, :, 1], cache_valid, scale
    )
    self_valid = jnp.ones((slots, 1), dtype=bool)
    self_state = state_each(
        grouped, new_kv[:, None, :, 0], new_kv[:, None, :, 1], self_valid, scale
    )
    first = first_slots(prompt_owner, response_counts)
    rank = jnp.clip(slot_index - first[chosen], 0, RESP - 1)
    entry = chosen * RESP + rank
    select = (
        (entry[None, :] == jnp.arange(prompt_count * RESP, dtype=jnp.int32)[:, None])
        & present[None, :]
    ).astype(jnp.float32)
    table = jnp.dot(
        select,
        queries.reshape(slots, query_heads * head_size).astype(jnp.float32),
        precision=lax.Precision.HIGHEST,
    )
    table = lax.psum(table, "dev").astype(jnp.bfloat16)
    table = table.reshape(prompt_count, RESP, local_heads, group, head_size)
    held = jnp.any(member, axis=0)
    first_prompt = jnp.sum((starts + lengths <= token_index[0]).astype(jnp.int32))
    reach = min(rows // PROMPT_MIN + 2, prompt_count)
    layout = (
        jnp.full((prompt_count, RESP, local_heads, group), -1e30, jnp.float32),
        jnp.zeros((prompt_count, RESP, local_heads, group), jnp.float32),
        jnp.zeros((prompt_count, RESP, local_heads, group, head_size), jnp.float32),
    )
    for step in range(reach):
        pick = jnp.minimum(first_prompt + step, prompt_count - 1)
        live = (first_prompt + step < prompt_count) & held[pick]
        reply_queries = lax.dynamic_index_in_dim(table, pick, 0, keepdims=False)
        reply_live = jnp.arange(RESP, dtype=jnp.int32) < response_counts[pick]
        row_member = (token_index >= starts[pick]) & (token_index < starts[pick] + lengths[pick])
        valid = live & reply_live[:, None] & row_member[None, :]
        fresh = state_shared(reply_queries, prompt_keys, prompt_values, valid, scale)
        earlier = tuple(
            (lax.dynamic_index_in_dim(part_now, pick, 0, keepdims=False) for part_now in layout)
        )
        merged = combine(earlier, fresh)
        layout = tuple(
            (
                lax.dynamic_update_index_in_dim(part_now, part_new, pick, 0)
                for part_now, part_new in zip(layout, merged)
            )
        )
    joined_peak, joined_total, joined_mixed = merged_2(layout, "dev", combine)
    flat_peak = joined_peak.reshape(prompt_count * RESP, local_heads, group)
    flat_total = joined_total.reshape(prompt_count * RESP, local_heads, group)
    flat_mixed = joined_mixed.reshape(prompt_count * RESP, local_heads, group, head_size)
    own_peak = jnp.take(flat_peak, entry, axis=0)
    own_total = jnp.take(flat_total, entry, axis=0)
    own_mixed = jnp.take(flat_mixed, entry, axis=0)
    prompt_state = (
        jnp.where(present[:, None, None], own_peak, -1e30),
        jnp.where(present[:, None, None], own_total, 0.0),
        jnp.where(present[:, None, None, None], own_mixed, 0.0),
    )
    final = combine(combine(prompt_state, cache_state), self_state)
    attended = (
        (final[2] / final[1][..., None]).reshape(slots, query_heads, head_size).astype(jnp.bfloat16)
    )
    flat = attended.reshape(slots, query_heads * head_size)
    weight_flat = out_weight.reshape(query_heads * head_size, out_weight.shape[2])
    head_terms = jnp.dot(
        lax.all_gather(flat, "dev", axis=0, tiled=True),
        weight_flat,
        preferred_element_type=jnp.float32,
    )
    block_out = lax.psum_scatter(head_terms, "role", scatter_dimension=0, tiled=True).astype(
        jnp.bfloat16
    )
    return (attended, block_out)


def solution(mesh):
    return jax.shard_map(
        on_device,
        mesh=mesh,
        in_specs=(
            P(("groups", "dev"), None),
            P(),
            P(None, "role", None, None),
            P("groups"),
            P("groups"),
            P("groups"),
            P(("groups", "dev"), "role", None),
            P(("groups", "dev"), "role", None, None),
            P(("groups", "dev"), None, "role", None, None),
            P(("groups", "dev")),
            P("role", None, "dev"),
        ),
        out_specs=(P(("groups", "dev"), "role", None), P(("groups", "role"), "dev")),
        check_vma=False,
    )
```

profile of v0, /device:TPU:0, one launch (start us, length us, event | category | flops | bytes accessed | tf_op | source)
XLA Modules:
  0.0 298.8 jit_solution(10407446676272909244)
XLA Ops:
  7.2 0.5 slice.31
  7.8 0.7 broadcast_add_fusion
  8.4 0.2 reduce-window.8
  8.6 1.9 bitcast_subtract_fusion.3
  11.8 0.7 broadcast_compare_fusion
  12.5 0.9 select_reduce_fusion.2
  13.4 1.3 fusion.107
  14.8 0.6 fusion.110
  16.3 0.7 fusion.109
  17.0 0.6 fusion.108
  17.6 0.7 add.228
  18.4 0.7 gather_fusion
  19.0 0.9 fusion.46
  19.9 79.5 %psum.7 = bf16[20,1024]{1,0:T(8,128)(2,1)S(1)} all-reduce(f32[20,1024]{1,0:T(8,128)S(1)} %fusion.46), channel_id=1, replica_groups=mesh['groups'=1,'role'=2,'dev'=16] {'dev'}, use_global_device_ids=true, to_apply=%region_9.10 | all-reduce | flops 20480 | bytes 122880 | tf_op jit(solution)/shard_map/psum | solution.py:156
  99.5 7.2 %reshape.412 = bf16[4096,512]{1,0:T(8,128)(2,1)} reshape(bf16[4096,2,2,128]{3,2,1,0:T(2,128)(2,1)} %param.17) | data formatting | bytes 8388608 | tf_op jit(solution)/shard_map/reshape | solution.py:125
  106.7 6.6 %copy.138 = bf16[512,4096]{1,0:T(8,128)(2,1)} copy(bf16[512,4096]{0,1:T(8,128)(2,1)} %bitcast.222) | data formatting | bytes 8388608 | tf_op jit(solution)/shard_map/dot_general | solution.py:123
  113.3 0.5 fusion.3
  113.8 3.6 %fusion.7 = f32[256,2,2,128]{0,3,2,1:T(8,128)S(1)} fusion(bf16[2,2,128,4096]{3,2,1,0:T(8,128)(2,1)} %bitcast.223, bf16[256,4096]{1,0:T(8,128)(2,1)S(1)} %copy-done.1, f32[4096]{0:T(1024)S(1)} %copy-done.7, f32[256]{0:T(256)S(1)} %add_rsqrt_fusion), kind=kOutput, calls=%fused_computation.18 | convolution fusion | flops 1077936128 | bytes 6833152 | tf_op jit(solution)/shard_map/dot_general | solution.py:123
  119.9 1.2 compare_and_fusion
  121.2 0.3 multiply_cosine_fusion
  122.0 0.6 compare_and_fusion.3
  122.8 0.2 fusion.112
  123.0 0.2 fusion.39
  123.2 0.2 fusion.30
  124.1 0.6 compare_and_fusion.1
  124.7 0.2 fusion.113
  125.0 0.2 fusion.27
  125.3 0.6 copy-done.2
  126.0 10.2 %fusion.106 = (bf16[16,256,2,1,128]{4,3,2,1,0:T(2,128)(2,1)}, bf16[16,256,2,1,128]{4,3,2,1,0:T(2,128)(2,1)}) fusion(bf16[16,256,2,2,128]{4,3,2,1,0:T(2,128)(2,1)} %param.23), kind=kLoop, calls=%fused_computation.189 | loop fusion | bytes 8388608 | tf_op jit(solution)/shard_map/slice | solution.py:138
  136.3 2.9 fusion.111
  139.4 0.1 fusion.59
  139.6 0.2 fusion.32
  139.9 0.2 fusion.41
  140.1 37.8 %all_gather.32 = f32[16,4,5,2,4]{2,4,3,1,0:T(4,128)S(1)} all-gather(f32[1,4,5,2,4]{2,4,3,1,0:T(4,128)S(1)} %get-tuple-element.219), channel_id=1, replica_groups=mesh['groups'=1,'role'=2,'dev'=16] {'dev'}, dimensions={0}, use_global_device_ids=true | all-gather | bytes 10880 | tf_op jit(solution)/shard_map/all_gather | solution.py:12
  177.9 38.5 %all_gather.29 = f32[16,4,5,2,4]{2,4,3,1,0:T(4,128)S(1)} all-gather(f32[1,4,5,2,4]{2,4,3,1,0:T(4,128)S(1)} %get-tuple-element.220), channel_id=1, replica_groups=mesh['groups'=1,'role'=2,'dev'=16] {'dev'}, dimensions={0}, use_global_device_ids=true | all-gather | bytes 10880 | tf_op jit(solution)/shard_map/all_gather | solution.py:12
  216.5 0.9 slice_bitcast_fusion.1
  217.4 22.4 %while.19 = (s32[]{:T(128)}, f32[4,5,2,4]{1,3,2,0:T(4,128)S(1)}, f32[4,5,2,4]{1,3,2,0:T(4,128)S(1)}, f32[4,5,2,4,128]{4,3,2,1,0:T(4,128)S(1)}, f32[16,4,5,2,4]{2...) while((s32[]{:T(128)}, f32[4,5,2,4]{1,3,2,0:T(4,128)S(1)}, ...), condition=%wide.region_15.16_spmd, body=%wide.region_14.15_spmd.sunk | while | flops 62405 | bytes 254871 | solution.py:17
  217.4 0.1 copy.236
  217.7 1.2 fusion.123
  218.9 0.1 copy.236
  219.2 1.2 fusion.123
  220.7 1.2 fusion.123
  222.2 1.2 fusion.123
  223.7 1.2 fusion.123
  225.2 1.2 fusion.123
  226.4 0.1 copy.236
  226.7 1.2 fusion.123
  227.9 0.1 copy.236
  228.2 1.2 fusion.123
  229.7 1.2 fusion.123
  231.2 1.2 fusion.123
  232.7 1.2 fusion.123
  234.2 1.2 fusion.123
  235.7 1.2 fusion.123
  237.2 1.2 fusion.123
  238.7 1.2 fusion.123
  240.0 0.6 gather_fusion.2
  240.8 0.6 gather_fusion.3
  242.1 0.6 gather_fusion.1
  242.7 2.7 fusion.24
  245.4 38.6 %all_gather.36 = bf16[256,1024]{1,0:T(8,128)(2,1)S(1)} all-gather(bf16[16,1024]{1,0:T(8,128)(2,1)S(1)} %convert_element_type.68), channel_id=1, replica_groups=mesh['groups'=1,'role'=2,'dev'=16] {'dev'}, dimensions={0}, use_global_device_ids=true | all-gather | bytes 557056 | tf_op jit(solution)/shard_map/all_gather | solution.py:203
  284.0 1.0 fusion.114
  285.1 5.3 %reduce-scatter.2.cloned.1.call-done = f32[128,256]{1,0:T(8,128)} async-done(((f32[256,256]{1,0:T(8,128)}), f32[128,256]{1,0:T(8,128)}) %reduce-scatter.2.cloned.1.call-update) | async-done | bytes 131088 | tf_op jit(solution)/shard_map/reduce_scatter | solution.py:207
  290.4 1.5 convert_element_type.69
  (116 shorter events, 6.6 us)
Async XLA Ops:
  7.2 276.9 %copy-start = (bf16[8,128,256]{2,1,0:T(8,128)(2,1)S(1)}, bf16[8,128,256]{2,1,0:T(8,128)(2,1)}, u32[]{:S(2)}) copy-start(bf16[8,128,256]{2,1,0:T(8,128)(2,1)} %param.25) | copy-start | bytes 1572868
  7.2 209.3 %all-gather.2.cloned.1.call-start = ((), (), s32[]{:S(2)}) async-start(), calls=%async_computation.1 | async-start | bytes 1392640 | tf_op jit(solution)/shard_map/all_gather | solution.py:12
  106.7 6.6 %copy-start.1 = (bf16[256,4096]{1,0:T(8,128)(2,1)S(1)}, bf16[256,4096]{1,0:T(8,128)(2,1)}, u32[]{:S(2)}) copy-start(bf16[256,4096]{1,0:T(8,128)(2,1)} %param.15) | copy-start | bytes 6291460
  106.7 7.1 %copy-start.7 = (f32[4096]{0:T(1024)S(1)}, f32[4096]{0:T(1024)}, u32[]{:S(2)}) copy-start(f32[4096]{0:T(1024)} %param.16) | copy-start | bytes 49156
  125.3 0.6 copy-start.2
  125.9 10.3 %copy-start.6 = (s32[16]{0:T(128)S(1)}, s32[16]{0:T(128)}, u32[]{:S(2)}) copy-start(s32[16]{0:T(128)} %param.24) | copy-start | bytes 196
  125.9 10.3 %copy-start.5 = (bf16[16,8,128]{2,1,0:T(8,128)(2,1)S(1)}, bf16[16,8,128]{2,1,0:T(8,128)(2,1)}, u32[]{:S(2)}) copy-start(bf16[16,8,128]{2,1,0:T(8,128)(2,1)} %param.21) | copy-start | bytes 98308
  126.0 13.4 %copy-start.3 = (bf16[16,2,2,128]{3,2,1,0:T(2,128)(2,1)S(1)}, bf16[16,2,2,128]{3,2,1,0:T(2,128)(2,1)}, u32[]{:S(2)}) copy-start(bf16[16,2,2,128]{3,2,1,0:T(2,128)(2,1)} %param.22) | copy-start | bytes 49156
  126.0 164.4 %reduce-scatter.2.cloned.1.call-start = ((), (), s32[]{:S(2)}) async-start(), calls=%async_computation.2 | async-start | bytes 393216 | tf_op jit(solution)/shard_map/reduce_scatter | solution.py:207
  245.4 46.5 %copy-start.4 = (bf16[16,2,4,128]{3,2,1,0:T(4,128)(2,1)}, bf16[16,2,4,128]{3,2,1,0:T(4,128)(2,1)S(1)}, u32[]{:S(2)}) copy-start(bf16[16,2,4,128]{3,2,1,0:T(4,128)(2,1)S(1)} %fusion.24) | copy-start | bytes 98308
Sparse Core Ops, SparseCore 0:
  126.1 53.9 all-gather.1
  285.2 5.1 reduce-scatter.1
where the time goes:
time: 300 us; the launch traced here: 299 us
  blocking collectives  194 us (65%)
  local copies, waits for them, and re-layouts  37.2 us (12%)
  other arithmetic  29.3 us (10%)
  between operations  20.1 us (7%)
  matrix products  12 us (4%)
  waiting for transfers between devices  5.37 us (2%)
    psum x1, blocking collectives, on_device(): table = lax.psum(table, 'dev').astype(jnp.bfloat16)  79.5 us
    all_gather x2, blocking collectives, merged_2(): gathered = jax.tree.map(lambda a: lax.all_gather(a, axis), part)  76.3 us
    all_gather x1, blocking collectives, on_device(): lax.all_gather(flat, 'dev', axis=0, tiled=True)  38.6 us
    add x15, other arithmetic, combine(): first[2] * left_scale[..., None] + second[2] * right_scale[..., None]  17.5 us
    slice x1, local copies, waits for them, and re-layouts, on_device(): response_cache[:, :, :, 0]  10.2 us
    reshape x1, local copies, waits for them, and re-layouts, on_device(): kv_weight.reshape(width, local_heads * 2 * head_size)  7.22 us
    dot_general x1, local copies, waits for them, and re-layouts, on_device(): jnp.dot(normed, kv_weight.reshape(width, local_heads * 2 * head_size), pr...  6.6 us
  transfers between devices with their start and end apart: 2, of which 1 were waited for; matrix products, arithmetic and copies ran while one was open for 5% of the time, Pallas kernels for 0%

commit v1 on v0

--- a/solution.py
+++ b/solution.py
@@ -1,3 +1,4 @@
+import functools
 import jax
 import jax.numpy as jnp
 from jax import lax
@@ -6,6 +7,14 @@
 RESP = 5
 PROMPT_MIN = 512
 rope_base = 500000.0
+
+
+def _name_streams(load, bus_axis):
+    low = lax.all_gather(load, bus_axis).sum(axis=0)
+    return low
+
+
+trails_end = functools.partial(_name_streams, bus_axis="dev")
 
 
 def merged_2(part, axis, combine):
@@ -153,7 +162,7 @@
         queries.reshape(slots, query_heads * head_size).astype(jnp.float32),
         precision=lax.Precision.HIGHEST,
     )
-    table = lax.psum(table, "dev").astype(jnp.bfloat16)
+    table = trails_end(table).astype(jnp.bfloat16)
     table = table.reshape(prompt_count, RESP, local_heads, group, head_size)
     held = jnp.any(member, axis=0)
     first_prompt = jnp.sum((starts + lengths <= token_index[0]).astype(jnp.int32))

time: 300 us -> 241 us (0.80)
  blocking collectives: 194 us -> 118 us
  waiting for transfers between devices: 5.37 us -> 24.1 us
  local copies, waits for them, and re-layouts: 37.2 us -> 34 us
    psum x1 -> x0, blocking collectives: 79.5 us -> none  [on_device(): table = lax.psum(table, 'dev').astype(jnp.bfloat16)]
    all_gather x0 -> x1, waiting for transfers between devices: none -> 20.3 us  [_name_streams(): low = lax.all_gather(load, bus_axis).sum(axis=0)]
    slice x1, local copies, waits for them, and re-layouts: 10.2 us -> 6.99 us  [on_device(): response_cache[:, :, :, 0]]
  transfers between devices with their start and end apart: 2 -> 3, of which waited for: 1 -> 2; matrix products, arithmetic and copies ran while one was open for 5% -> 16% of each run, Pallas kernels for 0% -> 0%
where the time goes in v1:
time: 241 us; the launch traced here: 240 us
  blocking collectives  118 us (49%)
  local copies, waits for them, and re-layouts  34 us (14%)
  other arithmetic  30.8 us (13%)
  waiting for transfers between devices  24.1 us (10%)
  between operations  19.8 us (8%)
  matrix products  12.8 us (5%)
    all_gather x2, blocking collectives, merged_2(): gathered = jax.tree.map(lambda a: lax.all_gather(a, axis), part)  77.4 us
    all_gather x1, blocking collectives, on_device(): lax.all_gather(flat, 'dev', axis=0, tiled=True)  40.4 us
    all_gather x1, waiting for transfers between devices, _name_streams(): low = lax.all_gather(load, bus_axis).sum(axis=0)  20.3 us
    add x15, other arithmetic, combine(): first[2] * left_scale[..., None] + second[2] * right_scale[..., None]  17.5 us
    reshape x1, local copies, waits for them, and re-layouts, on_device(): kv_weight.reshape(width, local_heads * 2 * head_size)  7.24 us
    slice x1, local copies, waits for them, and re-layouts, on_device(): response_cache[:, :, :, 0]  6.99 us
    dot_general x1, local copies, waits for them, and re-layouts, on_device(): jnp.dot(normed, kv_weight.reshape(width, local_heads * 2 * head_size), pr...  6.57 us
  transfers between devices with their start and end apart: 3, of which 2 were waited for; matrix products, arithmetic and copies ran while one was open for 16% of the time, Pallas kernels for 0%

profile of v1, /device:TPU:0, one launch (start us, length us, event | category | flops | bytes accessed | tf_op | source)
XLA Modules:
  0.0 239.8 jit_solution(860674896109455141)
XLA Ops:
  7.2 0.9 select_reduce_fusion.2
  8.1 0.7 add.226
  8.8 0.7 broadcast_compare_fusion
  9.6 0.7 gather_fusion
  10.3 1.5 convolution_bitcast_fusion
  11.9 0.5 slice.31
  12.4 0.7 broadcast_add_fusion
  13.1 0.2 reduce-window.8
  13.2 1.9 bitcast_subtract_fusion.3
  16.5 1.3 fusion.106
  17.8 0.6 fusion.109
  19.4 0.6 fusion.108
  20.0 0.6 fusion.107
  20.6 7.2 %reshape.412 = bf16[4096,512]{1,0:T(8,128)(2,1)} reshape(bf16[4096,2,2,128]{3,2,1,0:T(2,128)(2,1)} %param.17) | data formatting | bytes 8388608 | tf_op jit(solution)/shard_map/reshape | solution.py:134
  27.9 6.6 %copy.136 = bf16[512,4096]{1,0:T(8,128)(2,1)} copy(bf16[512,4096]{0,1:T(8,128)(2,1)} %bitcast.224) | data formatting | bytes 8388608 | tf_op jit(solution)/shard_map/dot_general | solution.py:132
  34.4 0.5 fusion.3
  37.4 1.2 compare_and_fusion
  39.2 0.6 compare_and_fusion.1
  39.9 0.3 multiply_cosine_fusion
  40.9 0.6 compare_and_fusion.3
  41.5 3.7 %fusion.7 = f32[256,2,2,128]{0,3,2,1:T(8,128)S(1)} fusion(bf16[2,2,128,4096]{3,2,1,0:T(8,128)(2,1)} %bitcast.225, bf16[256,4096]{1,0:T(8,128)(2,1)S(1)} %copy-done.2, f32[4096]{0:T(1024)S(1)} %copy-done.8, f32[256]{0:T(256)S(1)} %add_rsqrt_fusion), kind=kOutput, calls=%fused_computation.18 | convolution fusion | flops 1077936128 | bytes 6833152 | tf_op jit(solution)/shard_map/dot_general | solution.py:132
  45.4 7.0 %fusion.105 = (bf16[16,256,2,1,128]{4,3,2,1,0:T(2,128)(2,1)}, bf16[16,256,2,1,128]{4,3,2,1,0:T(2,128)(2,1)}) fusion(bf16[16,256,2,2,128]{4,3,2,1,0:T(2,128)(2,1)S(1)} %copy-done.1), kind=kLoop, calls=%fused_computation.189 | loop fusion | bytes 8388608 | tf_op jit(solution)/shard_map/slice | solution.py:147
  52.3 20.3 %all-gather.7.cloned.1.call-done = f32[16,20,1024]{2,1,0:T(8,128)} async-done(((f32[1,20,1024]{2,1,0:T(8,128)}), f32[16,20,1024]{2,1,0:T(8,128)}) %all-gather.7.cloned.1.call-update) | async-done | bytes 1310736 | tf_op jit(solution)/shard_map/all_gather | solution.py:13
  72.7 1.5 reduce_sum.111
  74.2 0.2 fusion.111
  74.5 0.2 fusion.39
  74.6 0.2 fusion.30
  74.9 0.2 fusion.112
  75.2 0.2 fusion.27
  75.4 0.6 copy-done.3
  76.2 2.9 %fusion.110 = (f32[16,2,4]{2,1,0:T(2,128)S(1)}, f32[16,2,4,256]{3,2,1,0:T(4,128)S(1)}) fusion(bf16[16,2,4,128]{3,2,1,0:T(4,128)(2,1)S(1)} %bitcast.234, bf16[16,256,2,1,128]{4,3,2,1,0:T(2,128)(2,1)} %get-tuple-element.211, pred[16,256]{1,0:T(8,128)(4,1)S(1)} %iota_compare_fusion), kind=kOutput, calls=%fused_computation.194 | convolution fusion | flops 8486784 | bytes 2265600 | tf_op jit(solution)/shard_map/sngd,slnd->sngl/dot_general | solution.py:81
  79.3 0.1 fusion.58
  79.6 0.2 fusion.32
  80.0 0.2 fusion.41
  80.2 40.4 %all_gather.40 = f32[16,4,5,2,4]{2,4,3,1,0:T(4,128)S(1)} all-gather(f32[1,4,5,2,4]{2,4,3,1,0:T(4,128)S(1)} %get-tuple-element.219), channel_id=1, replica_groups=mesh['groups'=1,'role'=2,'dev'=16] {'dev'}, dimensions={0}, use_global_device_ids=true | all-gather | bytes 10880 | tf_op jit(solution)/shard_map/all_gather | solution.py:21
  120.5 37.1 %all_gather.37 = f32[16,4,5,2,4]{2,4,3,1,0:T(4,128)S(1)} all-gather(f32[1,4,5,2,4]{2,4,3,1,0:T(4,128)S(1)} %get-tuple-element.220), channel_id=1, replica_groups=mesh['groups'=1,'role'=2,'dev'=16] {'dev'}, dimensions={0}, use_global_device_ids=true | all-gather | bytes 10880 | tf_op jit(solution)/shard_map/all_gather | solution.py:21
  157.6 0.9 slice_bitcast_fusion.1
  158.5 22.4 %while.19 = (s32[]{:T(128)}, f32[4,5,2,4]{1,3,2,0:T(4,128)S(1)}, f32[4,5,2,4]{1,3,2,0:T(4,128)S(1)}, f32[4,5,2,4,128]{4,3,2,1,0:T(4,128)S(1)}, f32[16,4,5,2,4]{2...) while((s32[]{:T(128)}, f32[4,5,2,4]{1,3,2,0:T(4,128)S(1)}, ...), condition=%wide.region_15.16_spmd, body=%wide.region_14.15_spmd.sunk | while | flops 62405 | bytes 254871 | solution.py:26
  158.8 1.2 fusion.122
  160.3 1.2 fusion.122
  161.8 1.2 fusion.122
  163.0 0.1 copy.234
  163.3 1.2 fusion.122
  164.8 1.2 fusion.122
  166.3 1.2 fusion.122
  167.8 1.2 fusion.122
  169.3 1.2 fusion.122
  170.8 1.2 fusion.122
  172.3 1.2 fusion.122
  173.8 1.2 fusion.122
  175.2 1.2 fusion.122
  176.5 0.1 copy.234
  176.7 1.2 fusion.122
  178.0 0.1 copy.234
  178.2 1.2 fusion.122
  179.7 1.2 fusion.122
  181.0 0.6 gather_fusion.2
  181.9 0.6 gather_fusion.3
  183.2 0.6 gather_fusion.1
  183.8 2.7 %fusion.24 = bf16[16,2,4,128]{3,2,1,0:T(4,128)(2,1)S(1)} fusion(bf16[16,256,2,1,128]{4,3,2,1,0:T(2,128)(2,1)} %get-tuple-element.212, f32[16,2,4,256]{3,2,1,0:T(4,128)S(1)} %get-tuple-element.244, f32[16,2,4]{2,1,0:T(2,128)S(1)} %get-tuple-element.243, f32[16,2,4,128]{3,2,1,0:T(4,128)S(1)} %gather_fusion.1, pred[16,256]{1,0:T(8,128)(4,1)S(1)} %iota_compare_fusion, ...), kind=kOutput, calls=%fused_computation.39 | convolution fusion | flops 8667136 | bytes 2350624 | tf_op jit(solution)/shard_map/sngl,slnd->sngd/dot_general | solution.py:83
  186.5 40.4 %all_gather.44 = bf16[256,1024]{1,0:T(8,128)(2,1)S(1)} all-gather(bf16[16,1024]{1,0:T(8,128)(2,1)S(1)} %convert_element_type.73), channel_id=1, replica_groups=mesh['groups'=1,'role'=2,'dev'=16] {'dev'}, dimensions={0}, use_global_device_ids=true | all-gather | bytes 557056 | tf_op jit(solution)/shard_map/all_gather | solution.py:212
  226.9 1.0 fusion.113
  228.0 3.8 %reduce-scatter.2.cloned.1.call-done = f32[128,256]{1,0:T(8,128)} async-done(((f32[256,256]{1,0:T(8,128)}), f32[128,256]{1,0:T(8,128)}) %reduce-scatter.2.cloned.1.call-update) | async-done | bytes 131088 | tf_op jit(solution)/shard_map/reduce_scatter | solution.py:216
  231.7 1.5 convert_element_type.74
  (121 shorter events, 6.8 us)
Async XLA Ops:
  7.2 219.8 %copy-start = (bf16[8,128,256]{2,1,0:T(8,128)(2,1)S(1)}, bf16[8,128,256]{2,1,0:T(8,128)(2,1)}, u32[]{:S(2)}) copy-start(bf16[8,128,256]{2,1,0:T(8,128)(2,1)} %param.25) | copy-start | bytes 1572868
  7.2 65.5 %all-gather.7.cloned.1.call-start = ((), (), s32[]{:S(2)}) async-start(), calls=%async_computation.3 | async-start | bytes 1671168 | tf_op jit(solution)/shard_map/all_gather | solution.py:13
  11.8 145.8 %all-gather.5.cloned.1.call-start = ((), (), s32[]{:S(2)}) async-start(), calls=%async_computation.1 | async-start | bytes 1392640 | tf_op jit(solution)/shard_map/all_gather | solution.py:21
  27.9 6.6 %copy-start.2 = (bf16[256,4096]{1,0:T(8,128)(2,1)S(1)}, bf16[256,4096]{1,0:T(8,128)(2,1)}, u32[]{:S(2)}) copy-start(bf16[256,4096]{1,0:T(8,128)(2,1)} %param.15) | copy-start | bytes 6291460
  27.9 13.7 %copy-start.8 = (f32[4096]{0:T(1024)S(1)}, f32[4096]{0:T(1024)}, u32[]{:S(2)}) copy-start(f32[4096]{0:T(1024)} %param.16) | copy-start | bytes 49156
  41.5 3.8 %copy-start.1 = (bf16[16,256,2,2,128]{4,3,2,1,0:T(2,128)(2,1)S(1)}, bf16[16,256,2,2,128]{4,3,2,1,0:T(2,128)(2,1)}, u32[]{:S(2)}) copy-start(bf16[16,256,2,2,128]{4,3,2,1,0:T(2,128)(2,1)} %param.23) | copy-start | bytes 12582916
  45.3 30.8 %copy-start.7 = (s32[16]{0:T(128)S(1)}, s32[16]{0:T(128)}, u32[]{:S(2)}) copy-start(s32[16]{0:T(128)} %param.24) | copy-start | bytes 196
  45.3 30.9 %copy-start.6 = (bf16[16,8,128]{2,1,0:T(8,128)(2,1)S(1)}, bf16[16,8,128]{2,1,0:T(8,128)(2,1)}, u32[]{:S(2)}) copy-start(bf16[16,8,128]{2,1,0:T(8,128)(2,1)} %param.21) | copy-start | bytes 98308
  52.3 26.9 %copy-start.4 = (bf16[16,2,2,128]{3,2,1,0:T(2,128)(2,1)S(1)}, bf16[16,2,2,128]{3,2,1,0:T(2,128)(2,1)}, u32[]{:S(2)}) copy-start(bf16[16,2,2,128]{3,2,1,0:T(2,128)(2,1)} %param.22) | copy-start | bytes 49156
  75.4 0.6 copy-start.3
  76.1 155.6 %reduce-scatter.2.cloned.1.call-start = ((), (), s32[]{:S(2)}) async-start(), calls=%async_computation.2 | async-start | bytes 393216 | tf_op jit(solution)/shard_map/reduce_scatter | solution.py:216
  186.5 46.8 %copy-start.5 = (bf16[16,2,4,128]{3,2,1,0:T(4,128)(2,1)}, bf16[16,2,4,128]{3,2,1,0:T(4,128)(2,1)S(1)}, u32[]{:S(2)}) copy-start(bf16[16,2,4,128]{3,2,1,0:T(4,128)(2,1)S(1)} %fusion.24) | copy-start | bytes 98308
Sparse Core Ops, SparseCore 0:
  11.9 60.6 all-gather.6
  76.2 56.6 all-gather.4
  228.1 3.5 reduce-scatter.1
